TPU v7x, 32 devices: a whole 2x2x4 slice. The times are simulated.
32 devices in a mesh: re: 4 (over y, x), ka: 8 (over z, core).
Axes of the slice: x: 2, y: 2, z: 4, core: 2. Of those that a mesh axis runs over, the one named last changes fastest.
Arguments:
- lattice_blocks: bfloat16 [192, 2, 3, 256], P(('re', 'ka')), may hold values from -0.4375 to 0.4375
- lattice_coords: int32 [192, 3], P(('re', 'ka')), may hold values from -8 to 8
- kpoint_index: int32 [192, 3], P('ka'), may hold values from 0 to 63
- polarization: float32 [3], replicated, may hold values from -4 to 4
- energy_gap: float32 [192, 32], P('ka'), may hold values from 0.5 to 2.5
- coupling: bfloat16 [8, 96, 2, 32, 8], P('ka', 're'), may hold values from -1 to 1
- phonon_weight: bfloat16 [8, 96], P('ka', 're'), may hold values from 0.19921875 to 5
Outputs:
- rates: float32 [192, 8], P('ka', 're')
All inputs are finite; a program needn't handle non-finite values.
Results may differ from a plain program's by a relative error of at most 0.0014.
Values may be sent and summed in bfloat16 or wider, within the bound.
A program may use at most 128 MiB of HBM per device.

v0:
```python
import math
import jax
import jax.numpy as jnp
from jax import lax
from jax.sharding import PartitionSpec as P

NV = 8
NC = 8
NMODE = 96
NKG = 64


def phase_rows(kpoint_index, coords):
    turns = jnp.mod(jnp.sum(kpoint_index[:, None, :] * coords[None, :, :], axis=2), NKG)
    angle = turns.astype(jnp.float32) * (2.0 * math.pi / NKG)
    cosine = jnp.cos(angle).astype(jnp.bfloat16)
    sine = jnp.sin(angle).astype(jnp.bfloat16)
    count = kpoint_index.shape[0]
    upper = jnp.stack([cosine, -sine], axis=2).reshape(count, -1)
    lower = jnp.stack([sine, cosine], axis=2).reshape(count, -1)
    return jnp.concatenate([upper, lower], axis=0)


def left_factor(momenta, polarization, energy_gap):
    count = momenta.shape[1]
    parts = momenta.reshape(2, count, 3, NV, -1)
    along = (
        parts[:, :, 0] * polarization[0]
        + parts[:, :, 1] * polarization[1]
        + parts[:, :, 2] * polarization[2]
    )
    return (along / energy_gap[None, :, None, :]).astype(jnp.bfloat16).reshape(2, count * NV, -1)


def rate_block(factor, coup, weight):

    def product(left, right):
        return jnp.einsum("qvmj,am->qvja", right, left, preferred_element_type=jnp.float32)

    real_left, imag_left = (factor[0], factor[1])
    real_right, imag_right = (coup[:, :, 0], coup[:, :, 1])
    are = product(real_left, real_right) - product(imag_left, imag_right)
    aim = product(real_left, imag_right) + product(imag_left, real_right)
    power = (are * are + aim * aim) * weight.astype(jnp.float32)[:, :, None, None]
    summed = jnp.sum(power, axis=(1, 2))
    count = factor.shape[1] // NV
    qcount = coup.shape[0]
    return jnp.sum(summed.reshape(qcount, count, NV), axis=2).T * (1.0 / (NMODE * NV * NC))


def body(
    lattice_blocks, lattice_coords, kpoint_index, polarization, energy_gap, coupling, phonon_weight
):
    own_count = kpoint_index.shape[0]
    cols = lattice_blocks.shape[2] * lattice_blocks.shape[3]
    blocks = lax.all_gather(lattice_blocks, "ka", axis=0, tiled=True)
    coords = lax.all_gather(lattice_coords.astype(jnp.bfloat16), "ka", axis=0, tiled=True)
    left = phase_rows(kpoint_index, coords.astype(jnp.int32))
    partial_value = jnp.dot(left, blocks.reshape(-1, cols), preferred_element_type=jnp.float32)
    momenta = lax.psum(partial_value, "re").reshape(2, own_count, cols)
    factor = left_factor(momenta, polarization, energy_gap)
    partial_rates = rate_block(
        factor,
        lax.all_gather(coupling, "ka", axis=0, tiled=True),
        lax.all_gather(phonon_weight, "ka", axis=0, tiled=True),
    )
    return lax.psum_scatter(partial_rates, "re", scatter_dimension=1, tiled=True)


def solution(mesh):
    return jax.shard_map(
        body,
        mesh=mesh,
        in_specs=(
            P(("re", "ka"), None, None, None),
            P(("re", "ka"), None),
            P("ka", None),
            P(),
            P("ka", None),
            P("ka", "re", None, None, None),
            P("ka", "re"),
        ),
        out_specs=P("ka", "re"),
        check_vma=False,
    )
```

profile of v0, /device:TPU:0, one launch (start us, length us, event | category | flops | bytes accessed | tf_op | source)
XLA Modules:
  0.0 103.5 jit_solution(17837021338715821611)
XLA Ops:
  6.5 0.0 all-reduce.3.cloned.1.call-start
  6.5 0.7 convert_bitcast_fusion
  7.2 13.5 %all-gather = bf16[8,6,3]{1,2,0:T(4,128)(2,1)S(1)} all-gather(bf16[1,6,3]{1,2,0:T(4,128)(2,1)S(1)} %convert_bitcast_fusion), channel_id=1, replica_groups=mesh['re'=4,'ka'=8] {'ka'}, dimensions={0}, use_global_device_ids=true | all-gather | bytes 324 | tf_op jit(solution)/shard_map/all_gather | solution.py:57
  20.7 0.1 reshape.103
  20.8 0.8 multiply_reduce_fusion.1
  21.5 0.1 fusion.16
  21.6 0.1 cosine_convert_fusion
  21.7 0.1 copy.53
  21.8 0.1 copy.54
  21.9 14.2 %all_gather.13 = bf16[48,2,3,256]{3,1,2,0:T(2,128)(2,1)S(1)} all-gather(bf16[6,2,3,256]{3,1,2,0:T(2,128)(2,1)} %param.7), channel_id=1, replica_groups=mesh['re'=4,'ka'=8] {'ka'}, dimensions={0}, use_global_device_ids=true | all-gather | bytes 165888 | tf_op jit(solution)/shard_map/all_gather | solution.py:56
  36.1 0.1 copy.55
  36.2 0.0 copy-start
  36.2 0.3 fusion.8
  36.5 0.2 reshape_reshape.3
  36.7 0.0 copy-start.3
  36.7 0.0 copy-start.4
  36.7 0.0 copy-start.2
  36.8 0.0 copy-start.1
  36.8 0.8 copy.56
  37.6 0.0 all-reduce.3.cloned.1.call-update
  37.6 0.0 copy-done
  37.7 16.3 %all_gather.14 = bf16[8,24,2,32,8]{3,1,4,0,2:T(8,128)(2,1)S(1)} all-gather(bf16[1,24,2,32,8]{3,1,4,0,2:T(8,128)(2,1)S(1)} %copy.57), channel_id=1, replica_groups=mesh['re'=4,'ka'=8] {'ka'}, dimensions={0}, use_global_device_ids=true | all-gather | bytes 221184 | tf_op jit(solution)/shard_map/all_gather | solution.py:64
  53.9 0.0 copy-done.3
  53.9 8.7 %all-gather.1 = bf16[8,1,24]{2,1,0:T(2,128)(2,1)S(1)} all-gather(bf16[1,1,24]{2,1,0:T(2,128)(2,1)S(1)} %bitcast.62), channel_id=1, replica_groups=mesh['re'=4,'ka'=8] {'ka'}, dimensions={0}, use_global_device_ids=true | all-gather | bytes 432 | tf_op jit(solution)/shard_map/all_gather | solution.py:65
  62.7 0.0 copy-done.4
  62.7 0.6 dynamic-slice
  63.9 0.0 copy-done.2
  63.9 0.6 fusion.17
  64.6 17.4 %all-reduce.3.cloned.1.call-done = f32[2,24,3,8,32]{4,3,1,0,2:T(8,128)} async-done(((f32[2,24,3,8,32]{4,3,1,0,2:T(8,128)}), f32[2,24,3,8,32]{4,3,1,0,2:T(8,128)}) %all-reduce.3.cloned.1.call-update) | async-done | bytes 147472 | tf_op jit(solution)/shard_map/psum | solution.py:60
  82.0 0.0 copy-done.1
  82.0 3.1 %fusion.7 = bf16[2,24,8,32]{3,2,1,0:T(8,128)(2,1)S(1)} fusion(f32[2,24,3,8,32]{4,3,1,0,2:T(8,128)} %all-reduce.3.cloned.1.call-done, f32[24,32]{1,0:T(8,128)S(1)} %copy-done.1, f32[]{:T(128)} %bitcast.6, f32[]{:T(128)} %bitcast.5, f32[]{:T(128)} %bitcast.4), kind=kLoop, calls=%fused_computation.13 | loop fusion | flops 86016 | bytes 175116 | tf_op jit(solution)/shard_map/convert_element_type | solution.py:32
  85.1 0.4 fusion
  85.5 0.4 fusion.2
  85.9 0.4 fusion.1
  86.3 0.7 multiply_reduce_fusion
  87.0 0.1 reshape.98
  87.1 0.1 reduce_sum.35
  87.2 8.9 %all-reduce = f32[24,8]{0,1:T(8,128)S(1)} all-reduce(f32[24,8]{0,1:T(8,128)S(1)} %multiply_bitcast_fusion), channel_id=2, replica_groups=mesh['re'=4,'ka'=8] {'re'}, use_global_device_ids=true, to_apply=%region_4.5.clone | all-reduce | flops 192 | bytes 1536
  96.1 0.6 constant_dynamic-slice_fusion
  (6 shorter events, 0.1 us)
Async XLA Ops:
  6.5 75.5 %all-reduce.3.cloned.1.call-start = ((), (), s32[]{:S(2)}) async-start(), calls=%async_computation | async-start | bytes 1179648 | tf_op jit(solution)/shard_map/psum | solution.py:60
  36.2 1.4 %copy-start = (bf16[1,24,2,32,8]{3,4,2,1,0:T(8,128)(2,1)S(1)}, bf16[1,24,2,32,8]{3,4,2,1,0:T(8,128)(2,1)}, u32[]{:S(2)}) copy-start(bf16[1,24,2,32,8]{3,4,2,1,0:T(8,128)(2,1)} %param.12) | copy-start | bytes 73732
  36.7 17.2 %copy-start.3 = (bf16[1,24]{1,0:T(2,128)(2,1)S(1)}, bf16[1,24]{1,0:T(2,128)(2,1)}, u32[]{:S(2)}) copy-start(bf16[1,24]{1,0:T(2,128)(2,1)} %param.13) | copy-start | bytes 148
  36.7 25.9 %copy-start.4 = (u32[32]{0:T(128)S(1)}, u32[32]{0:T(128)}, u32[]{:S(2)}) copy-start(u32[32]{0:T(128)} %constant.28) | copy-start | bytes 388
  36.7 27.2 %copy-start.2 = (f32[3]{0:T(128)S(1)}, f32[3]{0:T(128)}, u32[]{:S(2)}) copy-start(f32[3]{0:T(128)} %param.10) | copy-start | bytes 40
  36.8 45.3 %copy-start.1 = (f32[24,32]{1,0:T(8,128)S(1)}, f32[24,32]{1,0:T(8,128)}, u32[]{:S(2)}) copy-start(f32[24,32]{1,0:T(8,128)} %param.11) | copy-start | bytes 9220
Sparse Core Ops, SparseCore 0:
  37.8 44.1 all-reduce.2
where the time goes:
time: 104 us
  blocking collectives  61.6 us (59%)
  waiting for transfers between devices  17.5 us (17%)
  between operations  14.2 us (14%)
  other arithmetic  4.75 us (5%)
  local copies, waits for them, and re-layouts  3.38 us (3%)
  matrix products  2.13 us (2%)
    psum x1, waiting for transfers between devices, body(): momenta = lax.psum(partial_value, 're').reshape(2, own_count, cols)  17.4 us
    all_gather x1, blocking collectives, body(): lax.all_gather(coupling, 'ka', axis=0, tiled=True)  16.3 us
    all_gather x1, blocking collectives, body(): blocks = lax.all_gather(lattice_blocks, 'ka', axis=0, tiled=True)  14.2 us
    all_gather x1, blocking collectives, body(): lax.all_gather(lattice_coords.astype(jnp.bfloat16), 'ka', axis=0, tiled=T...  13.5 us
    unnamed x1, blocking collectives  8.93 us
    all_gather x1, blocking collectives, body(): lax.all_gather(phonon_weight, 'ka', axis=0, tiled=True)  8.72 us
    convert_element_type x1, other arithmetic, left_factor(): (along / energy_gap[None, :, None, :]).astype(jnp.bfloat16)  3.05 us
  transfers between devices with their start and end apart: 1, of which 1 were waited for; matrix products, arithmetic and copies ran while one was open for 1% of the time, Pallas kernels for 0%

commit v1 on v0

--- a/solution.py
+++ b/solution.py
@@ -57,7 +57,7 @@
     coords = lax.all_gather(lattice_coords.astype(jnp.bfloat16), "ka", axis=0, tiled=True)
     left = phase_rows(kpoint_index, coords.astype(jnp.int32))
     partial_value = jnp.dot(left, blocks.reshape(-1, cols), preferred_element_type=jnp.float32)
-    momenta = lax.psum(partial_value, "re").reshape(2, own_count, cols)
+    momenta = jnp.sum(lax.all_gather(partial_value, "re"), axis=0).reshape(2, own_count, cols)
     factor = left_factor(momenta, polarization, energy_gap)
     partial_rates = rate_block(
         factor,

time: 104 us -> 81.4 us (0.78)
  waiting for transfers between devices: 17.5 us -> 0 us
  between operations: 14.2 us -> 0.83 us
  blocking collectives: 61.6 us -> 72 us
  other arithmetic: 4.75 us -> 3.67 us
    psum x1 -> x0, waiting for transfers between devices: 17.4 us -> none  [body(): momenta = lax.psum(partial_value, 're').reshape(2, own_count, cols)]
    all_gather x0 -> x1, blocking collectives: none -> 10.8 us  [body(): lax.all_gather(partial_value, 're')]
    convert_element_type x1, other arithmetic: 3.05 us -> 1.95 us  [left_factor(): (along / energy_gap[None, :, None, :]).astype(jnp.bfloat16)]
  transfers between devices with their start and end apart: 1 -> 0, of which waited for: 1 -> 0; matrix products, arithmetic and copies ran while one was open for 1% -> 0% of each run, Pallas kernels for 0% -> 0%
where the time goes in v1:
time: 81.4 us; the launch traced here: 81.1 us
  blocking collectives  72 us (88%)
  other arithmetic  3.67 us (5%)
  local copies, waits for them, and re-layouts  2.53 us (3%)
  matrix products  2.12 us (3%)
  between operations  0.83 us (1%)
    all_gather x1, blocking collectives, body(): lax.all_gather(coupling, 'ka', axis=0, tiled=True)  15.7 us
    all_gather x1, blocking collectives, body(): blocks = lax.all_gather(lattice_blocks, 'ka', axis=0, tiled=True)  14.2 us
    all_gather x1, blocking collectives, body(): lax.all_gather(lattice_coords.astype(jnp.bfloat16), 'ka', axis=0, tiled=T...  13.5 us
    all_gather x1, blocking collectives, body(): lax.all_gather(partial_value, 're')  10.8 us
    unnamed x1, blocking collectives  8.97 us
    all_gather x1, blocking collectives, body(): lax.all_gather(phonon_weight, 'ka', axis=0, tiled=True)  8.77 us
    convert_element_type x1, other arithmetic, left_factor(): (along / energy_gap[None, :, None, :]).astype(jnp.bfloat16)  1.95 us
    dot_general x4, matrix products, product(): jnp.einsum('qvmj,am->qvja', right, left, preferred_element_type=jnp.float32)  1.86 us

profile of v1, /device:TPU:0, one launch (start us, length us, event | category | flops | bytes accessed | tf_op | source)
XLA Modules:
  0.0 81.1 jit_solution(11116556980021993344)
XLA Ops:
  0.0 0.7 convert_bitcast_fusion
  0.7 13.5 %all-gather.1 = bf16[8,6,3]{1,2,0:T(4,128)(2,1)S(1)} all-gather(bf16[1,6,3]{1,2,0:T(4,128)(2,1)S(1)} %convert_bitcast_fusion), channel_id=1, replica_groups=mesh['re'=4,'ka'=8] {'ka'}, dimensions={0}, use_global_device_ids=true | all-gather | bytes 324 | tf_op jit(solution)/shard_map/all_gather | solution.py:57
  14.2 0.1 reshape.104
  14.2 0.8 multiply_reduce_fusion.1
  15.0 0.1 fusion.16
  15.1 0.1 cosine_convert_fusion
  15.2 0.1 copy.48
  15.3 0.1 copy.49
  15.4 14.2 %all_gather.19 = bf16[48,2,3,256]{3,1,2,0:T(2,128)(2,1)S(1)} all-gather(bf16[6,2,3,256]{3,1,2,0:T(2,128)(2,1)} %param.7), channel_id=1, replica_groups=mesh['re'=4,'ka'=8] {'ka'}, dimensions={0}, use_global_device_ids=true | all-gather | bytes 165888 | tf_op jit(solution)/shard_map/all_gather | solution.py:56
  29.6 0.0 copy-start.2
  29.6 0.0 copy-start.1
  29.6 0.1 copy.50
  29.7 0.0 copy-start
  29.7 0.3 fusion.8
  30.0 10.8 %all-gather = f32[192,768]{1,0:T(8,128)S(1)} all-gather(f32[48,768]{1,0:T(8,128)S(1)} %fusion.8), channel_id=2, replica_groups=mesh['re'=4,'ka'=8] {'re'}, dimensions={0}, use_global_device_ids=true | all-gather | bytes 737280 | tf_op jit(solution)/shard_map/all_gather | solution.py:60
  40.8 0.2 reshape_reshape.3
  41.1 0.0 copy-done.2
  41.1 0.7 fusion.17
  41.7 0.0 copy-done.1
  41.7 1.9 %fusion.7 = bf16[2,24,8,32]{3,2,1,0:T(8,128)(2,1)S(1)} fusion(f32[2,24,3,8,32]{4,3,2,1,0:T(8,128)S(1)} %reshape_reshape.3, f32[24,32]{1,0:T(8,128)S(1)} %copy-done.1, f32[]{:T(128)} %bitcast.7, f32[]{:T(128)} %bitcast.6, f32[]{:T(128)} %bitcast.5), kind=kLoop, calls=%fused_computation.13 | loop fusion | flops 86016 | bytes 175116 | tf_op jit(solution)/shard_map/convert_element_type | solution.py:32
  43.7 0.0 copy-done
  43.7 15.7 %all_gather.22 = bf16[8,24,2,32,8]{3,1,4,0,2:T(8,128)(2,1)S(1)} all-gather(bf16[1,24,2,32,8]{3,1,4,0,2:T(8,128)(2,1)S(1)} %copy.51), channel_id=1, replica_groups=mesh['re'=4,'ka'=8] {'ka'}, dimensions={0}, use_global_device_ids=true | all-gather | bytes 221184 | tf_op jit(solution)/shard_map/all_gather | solution.py:64
  59.5 0.4 fusion
  59.9 0.0 copy-start.3
  59.9 0.4 fusion.2
  60.3 0.4 fusion.1
  60.7 0.0 copy-done.3
  60.7 8.8 %all-gather.2 = bf16[8,1,24]{2,1,0:T(2,128)(2,1)S(1)} all-gather(bf16[1,1,24]{2,1,0:T(2,128)(2,1)S(1)} %bitcast.64), channel_id=1, replica_groups=mesh['re'=4,'ka'=8] {'ka'}, dimensions={0}, use_global_device_ids=true | all-gather | bytes 432 | tf_op jit(solution)/shard_map/all_gather | solution.py:65
  69.5 0.0 copy-start.4
  69.5 0.7 multiply_reduce_fusion
  70.1 0.1 reshape.98
  70.2 0.1 reduce_sum.45
  70.4 9.0 %all-reduce = f32[24,8]{0,1:T(8,128)S(1)} all-reduce(f32[24,8]{0,1:T(8,128)S(1)} %multiply_bitcast_fusion), channel_id=3, replica_groups=mesh['re'=4,'ka'=8] {'re'}, use_global_device_ids=true, to_apply=%region_4.5.clone | all-reduce | flops 192 | bytes 1536
  79.3 0.0 copy-done.4
  79.3 0.6 dynamic-slice
  80.6 0.6 constant_dynamic-slice_fusion
  (7 shorter events, 0.1 us)
Async XLA Ops:
  29.6 11.5 %copy-start.2 = (f32[3]{0:T(128)S(1)}, f32[3]{0:T(128)}, u32[]{:S(2)}) copy-start(f32[3]{0:T(128)} %param.10) | copy-start | bytes 40
  29.6 12.1 %copy-start.1 = (f32[24,32]{1,0:T(8,128)S(1)}, f32[24,32]{1,0:T(8,128)}, u32[]{:S(2)}) copy-start(f32[24,32]{1,0:T(8,128)} %param.11) | copy-start | bytes 9220
  29.7 14.0 %copy-start = (bf16[1,24,2,32,8]{3,4,2,1,0:T(8,128)(2,1)S(1)}, bf16[1,24,2,32,8]{3,4,2,1,0:T(8,128)(2,1)}, u32[]{:S(2)}) copy-start(bf16[1,24,2,32,8]{3,4,2,1,0:T(8,128)(2,1)} %param.12) | copy-start | bytes 73732
  59.9 0.8 %copy-start.3 = (bf16[1,24]{1,0:T(2,128)(2,1)S(1)}, bf16[1,24]{1,0:T(2,128)(2,1)}, u32[]{:S(2)}) copy-start(bf16[1,24]{1,0:T(2,128)(2,1)} %param.13) | copy-start | bytes 148
  69.5 9.9 %copy-start.4 = (u32[32]{0:T(128)S(1)}, u32[32]{0:T(128)}, u32[]{:S(2)}) copy-start(u32[32]{0:T(128)} %constant.28) | copy-start | bytes 388
